TPU v7x, 256 devices: a whole 4x4x8 slice. The times are simulated.
256 devices in a mesh: scen: 64 (over z_hi, x, y, core), col: 4 (over z_lo).
Axes of the slice: x: 4, y: 4, z: 8 (z_hi: 2, z_lo: 4; z = z_hi * 4 + z_lo), core: 2. Of those that a mesh axis runs over, the one named last changes fastest.
Arguments:
- coef: float32 [32768, 8192], P('scen', 'col'), as said below
- mask: int32 [32768], replicated, may hold values from 0 to 1, as said below
- assign: int32 [4096], replicated, may hold values from 0 to 4095, each once
Outputs:
- master: float32 [4, 2048, 32768], P('col', 'scen')
Inputs may be any that keep to these rules, and one draw needn't show every extreme that they name: `mask`: in each aligned block of 512 cuts (the cuts of one index of scen) exactly 256 are active. `coef`: magnitudes of rows and of columns differ widely; entries are finite and not zero on every row.
All inputs are finite; a program needn't handle non-finite values.
Results may differ from a plain program's by a relative error of at most 0.00007.
Values sent between devices are 32-bit elements; how exact they have to be, the bound alone decides.
A program may use at most 128 MiB of HBM per device.

v0:
```python
import jax
import jax.numpy as jnp
from jax import lax
from jax.sharding import PartitionSpec as P

NV = 8192
K = 8
ACT_DEV = 256


EPS = 1e-06


def copy_for_each(shard, axis):
    copies = jnp.broadcast_to(shard, (lax.axis_size(axis), *shard.shape))
    return lax.all_to_all(copies, axis, split_axis=0, concat_axis=0, tiled=True)


def of_everyone(shard, axis):
    everything = copy_for_each(shard, axis)
    return jnp.sum(everything, axis=0)


def on_device(coef, mask, assign):
    rows, width = coef.shape
    groups = lax.axis_size("scen")
    slice_width = width // groups
    cut_total = groups * rows
    slot_total = cut_total // K
    active_total = ACT_DEV * groups
    partial_value = jnp.sum(coef * coef, axis=1)
    total = of_everyone(partial_value, "col")
    row_norm = jnp.sqrt(total / NV + EPS)
    device_index = lax.axis_index("scen")
    own_mask = lax.dynamic_slice_in_dim(mask, device_index * rows, rows)
    live = own_mask.astype(jnp.float32)
    scaled = coef / row_norm[:, None] * live[:, None]
    flipped = scaled.T.reshape(groups, slice_width, rows)
    inverse = jnp.argsort(assign, stable=True)
    block = lax.all_to_all(flipped, "scen", split_axis=0, concat_axis=2, tiled=True)
    norm = jnp.sqrt(jnp.sum(block * block, axis=2, keepdims=True) / active_total + EPS)
    arrived = block / norm
    slotted = arrived.reshape(1, slice_width, slot_total, K)
    return jnp.take(slotted, inverse, axis=2).reshape(1, slice_width, cut_total)


def solution(mesh):
    in_specs = (P("scen", "col"), P(), P())
    out_specs = P("col", "scen", None)
    return jax.shard_map(
        on_device, mesh=mesh, in_specs=in_specs, out_specs=out_specs, check_vma=False
    )
```

profile of v0, /device:TPU:38, one launch (start us, length us, event | category | flops | bytes accessed | tf_op | source)
XLA Modules:
  0.0 222.7 jit_solution(7704040456454407680)
XLA Ops:
  0.0 2.5 %multiply_reduce_fusion.1 = f32[512]{0:T(512)S(1)} fusion(f32[512,2048]{1,0:T(8,128)} %param.3), kind=kLoop, calls=%fused_computation.5 | loop fusion | flops 2096640 | bytes 4196352 | tf_op jit(solution)/shard_map/reduce_sum | solution.py:31
  2.5 0.6 broadcast_in_dim.25
  3.1 6.0 %all-to-all-start = ((f32[4,1,512]{2,1,0:T(1,128)}), f32[4,1,512]{2,1,0:T(1,128)S(1)}, u32[]{:S(2)}, u32[]{:S(2)}) async-start(f32[4,1,512]{2,1,0:T(1,128)} %broadcast_in_dim.25), calls=%async_computation | async-start | bytes 16384 | tf_op jit(solution)/shard_map/all_to_all | solution.py:16
  9.1 0.8 dynamic-slice_convert_fusion
  9.9 5.3 %copy.11 = f32[512,2048]{0,1:T(8,128)} copy(f32[512,2048]{1,0:T(8,128)} %param.3) | data formatting | bytes 8388608 | tf_op args[0]
  15.2 0.0 all-to-all-done
  15.3 4.8 %divide_multiply_fusion = f32[512,2048]{0,1:T(8,128)} fusion(f32[512,2048]{0,1:T(8,128)} %copy.11, f32[512]{0:T(512)S(1)} %dynamic-slice_convert_fusion, f32[512]{0:T(512)S(1)} %add_sqrt_fusion), kind=kLoop, calls=%fused_computation.4 | loop fusion | flops 2097152 | bytes 8392704 | tf_op jit(solution)/shard_map/mul | solution.py:37
  20.1 0.0 copy-start
  20.1 12.3 %all-to-all-start.1 = ((f32[64,32,512]{2,1,0:T(8,128)}), f32[64,32,512]{2,1,0:T(8,128)}, u32[]{:S(2)}, u32[]{:S(2)}) async-start(f32[64,32,512]{2,1,0:T(8,128)} %bitcast.15), calls=%async_computation.1 | async-start | bytes 8388608 | tf_op jit(solution)/shard_map/all_to_all | solution.py:40
  32.4 0.0 copy-done
  32.4 5.8 %sort.17 = (s32[4096]{0:T(1024)}, s32[4096]{0:T(1024)S(1)}) sort(s32[4096]{0:T(1024)S(1)} %copy-done, s32[4096]{0:T(1024)S(1)} %iota.4), dimensions={0}, to_apply=%region_0.0 | sort | flops 49152 | bytes 65536 | tf_op jit(solution)/shard_map/jit(argsort)/sort | solution.py:39
  38.1 2.1 broadcast_in_dim.22
  40.3 1.1 broadcast_in_dim.23
  41.4 89.1 %all-to-all-done.1 = f32[64,32,512]{2,1,0:T(8,128)} async-done(((f32[64,32,512]{2,1,0:T(8,128)}), f32[64,32,512]{2,1,0:T(8,128)}, u32[]{:S(2)}, u32[]{:S(2)}) %all-to-all-start.1) | async-done | bytes 4194336 | tf_op jit(solution)/shard_map/all_to_all | solution.py:40
  130.5 10.5 %copy.12 = f32[1,32,64,512]{1,3,2,0:T(8,128)} copy(f32[1,32,64,512]{3,1,2,0:T(8,128)} %bitcast.3) | data formatting | bytes 8388608 | tf_op jit(solution)/shard_map/all_to_all | solution.py:40
  141.0 2.8 %multiply_reduce_fusion = f32[32]{0:T(128)S(1)} fusion(f32[64,32,512]{2,1,0:T(8,128)} %all-to-all-done.1), kind=kLoop, calls=%fused_computation.3 | loop fusion | flops 2097120 | bytes 4194432 | tf_op jit(solution)/shard_map/reduce_sum | solution.py:41
  143.8 11.3 %divide_bitcast_fusion = f32[32,4096,8]{0,2,1:T(8,128)} fusion(f32[1,32,4096,8]{1,3,2,0:T(8,128)} %bitcast.14, f32[32]{0:T(128)S(1)} %add_sqrt_fusion.1), kind=kLoop, calls=%fused_computation.2 | loop fusion | flops 1048576 | bytes 8388736 | tf_op jit(solution)/shard_map/div | solution.py:42
  155.0 36.9 %gather_fusion = f32[4096,32,8]{1,2,0:T(8,128)} fusion(f32[32,4096,8]{0,2,1:T(8,128)} %divide_bitcast_fusion, s32[4096]{0:T(1024)S(1)} %fusion), kind=kCustom, calls=%fused_computation | custom fusion | bytes 8404992 | tf_op jit(solution)/shard_map/jit(_take)/gather | solution.py:44
  192.0 19.1 %bitcast_select_fusion = f32[1,32,32768]{1,2,0:T(8,128)} fusion(f32[4096,32,8]{1,2,0:T(8,128)} %gather_fusion, pred[32768]{0:T(1024)(128)(4,1)S(1)} %broadcast_in_dim.23), kind=kLoop, calls=%fused_computation.1 | loop fusion | flops 1048576 | bytes 8421376 | tf_op jit(solution)/shard_map/jit(_take)/select_n | solution.py:44
  211.1 11.6 %copy.13 = f32[1,32,32768]{2,1,0:T(8,128)} copy(f32[1,32,32768]{1,2,0:T(8,128)} %bitcast_select_fusion) | data formatting | bytes 8388608 | tf_op jit(solution)/shard_map/jit(_take)/select_n | solution.py:44
  (6 shorter events, 0.1 us)
Async XLA Ops:
  3.1 12.1 %all-to-all-start = ((f32[4,1,512]{2,1,0:T(1,128)}), f32[4,1,512]{2,1,0:T(1,128)S(1)}, u32[]{:S(2)}, u32[]{:S(2)}) async-start(f32[4,1,512]{2,1,0:T(1,128)} %broadcast_in_dim.25), calls=%async_computation | async-start | bytes 16384 | tf_op jit(solution)/shard_map/all_to_all | solution.py:16
  20.1 12.3 %copy-start = (s32[4096]{0:T(1024)S(1)}, s32[4096]{0:T(1024)}, u32[]{:S(2)}) copy-start(s32[4096]{0:T(1024)} %param.5) | copy-start | bytes 49156
  20.1 110.5 %all-to-all-start.1 = ((f32[64,32,512]{2,1,0:T(8,128)}), f32[64,32,512]{2,1,0:T(8,128)}, u32[]{:S(2)}, u32[]{:S(2)}) async-start(f32[64,32,512]{2,1,0:T(8,128)} %bitcast.15), calls=%async_computation.1 | async-start | bytes 8388608 | tf_op jit(solution)/shard_map/all_to_all | solution.py:40
where the time goes:
time: 223 us
  waiting for transfers between devices  89.2 us (40%)
  local copies, waits for them, and re-layouts  68.2 us (31%)
  other arithmetic  47 us (21%)
  starting transfers between devices  18.3 us (8%)
    all_to_all x1, waiting for transfers between devices, on_device(): lax.all_to_all(flipped, 'scen', split_axis=0, concat_axis=2, tiled=True)  89.1 us
    gather x1, local copies, waits for them, and re-layouts, on_device(): return jnp.take(slotted, inverse, axis=2).reshape(1, slice_width, cut_total)  36.9 us
    select_n x1, other arithmetic, on_device(): return jnp.take(slotted, inverse, axis=2).reshape(1, slice_width, cut_total)  19.1 us
    all_to_all x1, starting transfers between devices, on_device(): lax.all_to_all(flipped, 'scen', split_axis=0, concat_axis=2, tiled=True)  12.3 us
    select_n x1, local copies, waits for them, and re-layouts, on_device(): return jnp.take(slotted, inverse, axis=2).reshape(1, slice_width, cut_total)  11.6 us
    div x1, other arithmetic, on_device(): arrived = block / norm  11.3 us
    all_to_all x1, local copies, waits for them, and re-layouts, on_device(): lax.all_to_all(flipped, 'scen', split_axis=0, concat_axis=2, tiled=True)  10.5 us
    all_to_all x1, starting transfers between devices, copy_for_each(): return lax.all_to_all(copies, axis, split_axis=0, concat_axis=0, tiled=True)  6 us
  transfers between devices with their start and end apart: 2, of which 1 were waited for; matrix products, arithmetic and copies ran while one was open for 7% of the time, Pallas kernels for 0%

commit v1 on v0

v1 whole, which is shorter than its diff:
```python
import functools

import jax
import jax.numpy as jnp
from jax import lax
from jax.experimental import pallas as pl
from jax.experimental.pallas import tpu as pltpu
from jax.sharding import PartitionSpec as P

NV = 8192
K = 8
ACT_DEV = 256
EPS = 1e-06

LANES = 128
PART = 32
QROWS = 64
HELD = QROWS + 8
N_SCEN = 64
COLS = 4
MESH = pl.DeviceIdType.MESH
F32 = jnp.float32
BF16 = jnp.bfloat16


def iota(shape, dim):
    return lax.broadcasted_iota(jnp.int32, shape, dim)


def ones_where(cond):
    return jnp.where(cond, 1.0, 0.0).astype(BF16)


def dot(a, b):
    return jnp.dot(a, b, preferred_element_type=F32)


def dot_nt(a, b):
    return lax.dot_general(
        a, b, (((1,), (1,)), ((), ())), preferred_element_type=F32
    )


def exchange_kernel(
    coef_ref,
    mask_ref,
    assign_ref,
    held_ref,
    inv_ref,
    tbl_ref,
    idx_ref,
    val_ref,
    coef_v,
    pick,
    dense,
    packed,
    part,
    slots,
    in_sem,
    csend,
    crecv,
    zsem,
    ssem,
    rsem,
):
    rows, width = coef_ref.shape
    me = lax.axis_index("scen")
    group = lax.axis_index("col")
    half = N_SCEN // 2
    zh = me // half
    chunk = 256
    n_chunks = width // chunk

    def load(e):
        cols = pl.ds(pl.multiple_of(e * chunk, chunk), chunk)
        return pltpu.make_async_copy(
            coef_ref.at[:, cols], coef_v.at[:, cols], in_sem.at[e]
        )

    for e in range(n_chunks):
        load(e).start()

    barrier = pltpu.get_barrier_semaphore()
    across = (me + half) % N_SCEN
    pl.semaphore_signal(
        barrier, inc=1, device_id={"scen": across}, device_id_type=MESH
    )
    for d in range(1, COLS):
        pl.semaphore_signal(
            barrier,
            inc=1,
            device_id={"col": (group + d) % COLS},
            device_id_type=MESH,
        )

    def greet(t, _):
        pl.semaphore_signal(
            barrier,
            inc=1,
            device_id={"scen": zh * half + (me + t) % half},
            device_id_type=MESH,
        )
        return 0

    lax.fori_loop(1, half, greet, 0)

    own = mask_ref[pl.ds(pl.multiple_of(me // 2 * 8, 8), 8), :].astype(F32)
    own = jnp.where(me % 2 == 1, pltpu.roll(own, 4, 0), own)
    before = ones_where(iota((LANES, LANES), 0) < iota((LANES, LANES), 1))
    rank = dot(own.astype(BF16), before)
    base = jnp.zeros((1, 1), F32)
    for k in range(rows // LANES):
        row = own[k : k + 1, :]
        here = (rank[k : k + 1, :] + base).astype(jnp.int32)
        here = jnp.where(row > 0.5, here, -1)
        pick[:, k * LANES : (k + 1) * LANES] = ones_where(
            iota((ACT_DEV, LANES), 0) == here
        )
        base = base + jnp.sum(row, axis=1, keepdims=True)

    def compact(e, acc):
        load(e).wait()
        cols = pl.ds(pl.multiple_of(e * chunk, chunk), chunk)
        x = coef_v[:, cols]
        hi = x.astype(BF16)
        rest = x - hi.astype(F32)
        mid = rest.astype(BF16)
        low = (rest - mid.astype(F32)).astype(BF16)
        sel = pick[...]
        z = dot(sel, hi) + dot(sel, mid) + dot(sel, low)
        dense[:, cols] = z
        for j in range(chunk // LANES):
            zj = z[:, j * LANES : (j + 1) * LANES]
            acc = acc + zj * zj
        return acc

    acc = lax.fori_loop(0, n_chunks, compact, jnp.zeros((ACT_DEV, LANES), F32))
    mine = jnp.sum(acc.T, axis=0, keepdims=True)
    part[group] = jnp.broadcast_to(mine, (8, ACT_DEV))

    pl.semaphore_wait(barrier, half - 1 + 1 + COLS - 1)

    def share(d):
        return pltpu.make_async_remote_copy(
            src_ref=part.at[group],
            dst_ref=part.at[group],
            send_sem=csend.at[d - 1],
            recv_sem=crecv.at[d - 1],
            device_id={"col": (group + d) % COLS},
            device_id_type=MESH,
        )

    for d in range(1, COLS):
        share(d).start()
    pl.semaphore_signal(zsem, inc=1, device_id={"scen": across}, device_id_type=MESH)
    for d in range(1, COLS):
        share(d).wait()
    total = part[0] + part[1] + part[2] + part[3]
    inv_row = 1.0 / jnp.sqrt(total[0:1, :] / NV + EPS)
    scale = jnp.broadcast_to(inv_row, (LANES, ACT_DEV)).T
    pl.semaphore_wait(zsem, 1)

    lane_group = iota((QROWS, LANES), 1) // PART

    def send(d):
        return pltpu.make_async_remote_copy(
            src_ref=packed.at[d],
            dst_ref=held_ref.at[me],
            send_sem=ssem.at[d],
            recv_sem=rsem.at[me],
            device_id={"scen": d},
            device_id_type=MESH,
        )

    n_tiles = width // LANES
    half_tiles = n_tiles // 2
    own_tile = (me % half) // 4

    def pack(i, _):
        e = ((1 - zh + i // half_tiles) % 2) * half_tiles + (own_tile + i) % half_tiles
        cols = pl.ds(pl.multiple_of(e * LANES, LANES), LANES)
        quarters = [
            dense[q * QROWS : (q + 1) * QROWS, cols]
            * scale[q * QROWS : (q + 1) * QROWS, :]
            for q in range(4)
        ]
        for f in range(4):
            out = None
            for q in range(4):
                shift = PART * (q - f) % LANES
                moved = pltpu.roll(quarters[q], shift, 1) if shift else quarters[q]
                out = moved if out is None else jnp.where(lane_group == q, moved, out)
            packed[4 * e + f] = out
        for f in range(4):
            d = 4 * e + (f + me) % 4

            @pl.when(d != me)
            def _():
                send(d).start()

        return 0

    lax.fori_loop(0, n_tiles, pack, 0)
    held_ref[me] = packed[me]

    count = jnp.zeros((32, LANES), F32)
    bits = jnp.zeros((32, LANES), F32)
    r_i, l_i = iota((LANES, LANES), 0), iota((LANES, LANES), 1)
    for a in range(8):
        m = mask_ref[pl.ds(a, 32, stride=8), :].astype(F32).astype(BF16)
        pool = jnp.where(l_i == 16 * a + r_i // K, 1.0, 0.0)
        weight = lax.shift_left(jnp.ones_like(r_i), r_i % K).astype(F32)
        count = count + dot(m, pool.astype(BF16))
        bits = bits + dot(m, (pool * weight).astype(BF16))
    first = dot(
        count.astype(BF16), ones_where((r_i < l_i) & (r_i // 64 == l_i // 64))
    ).astype(jnp.int32)
    to = assign_ref[...]
    source = 2 * iota((32, LANES), 0) + iota((32, LANES), 1) // 64
    quarter = lax.rem(lax.rem(to, 64) // 16 - first // QROWS + 8, 4)
    at = quarter * (N_SCEN * HELD) + source * HELD + lax.rem(first, QROWS)
    slots[0] = (to // 64).astype(F32)
    slots[1] = lax.rem(to, 64).astype(F32)
    slots[2] = (at // 256).astype(F32)
    slots[3] = lax.rem(at, 256).astype(F32)
    slots[4] = bits

    def place(k, acc):
        s_i = iota((64, LANES), 0).astype(F32)
        high = jnp.where(s_i == slots[0, pl.ds(k, 1), :], 1.0, 0.0)
        low = jnp.where(s_i == slots[1, pl.ds(k, 1), :], 1.0, 0.0).astype(BF16)
        return tuple(
            acc[j] + dot_nt((high * slots[2 + j, pl.ds(k, 1), :]).astype(BF16), low)
            for j in range(3)
        )

    zero = jnp.zeros((64, 64), F32)
    at_hi, at_lo, pattern = lax.fori_loop(0, 32, place, (zero, zero, zero))
    tbl_ref[...] = (at_hi * 256.0 + at_lo).astype(jnp.int32)
    k_i = lax.rem(iota((64, LANES), 1), K)
    for q in range(4):
        spread = ones_where(iota((64, LANES), 0) - 16 * q == iota((64, LANES), 1) // K)
        pat = dot(pattern.astype(BF16), spread).astype(jnp.int32)
        before_k = jnp.zeros((64, LANES), jnp.int32)
        own_bit = jnp.zeros((64, LANES), jnp.int32)
        for m in range(K):
            bit = lax.shift_right_logical(pat, m) & 1
            before_k = before_k + jnp.where(k_i > m, bit, 0)
            own_bit = own_bit + jnp.where(k_i == m, bit, 0)
        idx_ref[q] = iota((64, LANES), 1) - k_i + before_k
        val_ref[q] = own_bit.astype(F32)

    def take(t, acc):
        s = (me + t) % N_SCEN

        @pl.when(t > 0)
        def _():
            pltpu.make_async_remote_copy(
                src_ref=packed.at[s],
                dst_ref=held_ref.at[s],
                send_sem=ssem.at[s],
                recv_sem=rsem.at[s],
                device_id={"scen": s},
                device_id_type=MESH,
            ).wait_recv()

        x = held_ref[s]
        return acc + x * x

    acc = lax.fori_loop(0, N_SCEN, take, jnp.zeros((QROWS, LANES), F32))
    col = jnp.sum(acc, axis=0, keepdims=True)
    col = jnp.broadcast_to(col, (8, LANES))
    col = col + pltpu.roll(col, 64, 1)
    col = col + pltpu.roll(col, 32, 1)
    inv_ref[...] = 1.0 / jnp.sqrt(col / (ACT_DEV * N_SCEN) + EPS)

    def finish(t, _):
        d = (me + t) % N_SCEN

        send(d).wait_send()
        return 0

    lax.fori_loop(1, N_SCEN, finish, 0)


def place_kernel(per_step, tbl_ref, held_ref, inv_ref, idx_ref, val_ref, out_ref, turned):
    step = pl.program_id(0)

    @pl.when(step == 0)
    def _():
        inv = jnp.broadcast_to(inv_ref[0:1, :], (HELD, LANES))

        def turn(s, _):
            x = held_ref[s]
            x = jnp.concatenate([x, pltpu.roll(x[:8], LANES - PART, 1)], axis=0) * inv
            for p in range(4):
                y = pltpu.roll(x, PART * p, 1) if p else x
                turned[pl.ds(pl.multiple_of((p * N_SCEN + s) * HELD, 8), HELD), :] = y
            return 0

        lax.fori_loop(0, N_SCEN, turn, 0)

    lane_group = iota((8, LANES), 1) // PART

    def block(h, _):
        hi = step * per_step + h
        tiles = []
        for i in range(16):
            m = None
            for q in range(4):
                x = turned[pl.ds(tbl_ref[hi, 16 * q + i], 8), :]
                m = x if m is None else jnp.where(lane_group == q, x, m)
            tiles.append(m)
        flipped = jnp.concatenate(tiles, axis=0).T
        for q in range(4):
            idx = jnp.broadcast_to(idx_ref[q, pl.ds(hi, 1), :], (PART, LANES))
            val = jnp.broadcast_to(val_ref[q, pl.ds(hi, 1), :], (PART, LANES))
            y = flipped[q * PART : (q + 1) * PART, :]
            y = jnp.take_along_axis(y, idx, axis=1) * val
            out_ref[0, :, pl.ds(pl.multiple_of(h * 512 + q * LANES, LANES), LANES)] = y
        return 0

    lax.fori_loop(0, per_step, block, 0)


def on_device(coef, mask, assign):
    rows, width = coef.shape
    vmem = pl.BlockSpec(memory_space=pltpu.VMEM)
    held, inv, tbl, idx, val = pl.pallas_call(
        exchange_kernel,
        out_shape=(
            jax.ShapeDtypeStruct((N_SCEN, QROWS, LANES), F32),
            jax.ShapeDtypeStruct((8, LANES), F32),
            jax.ShapeDtypeStruct((64, 64), jnp.int32),
            jax.ShapeDtypeStruct((4, 64, LANES), jnp.int32),
            jax.ShapeDtypeStruct((4, 64, LANES), F32),
        ),
        in_specs=[pl.BlockSpec(memory_space=pltpu.HBM), vmem, vmem],
        out_specs=(vmem, vmem, vmem, vmem, vmem),
        scratch_shapes=[
            pltpu.VMEM((rows, width), F32),
            pltpu.VMEM((ACT_DEV, rows), BF16),
            pltpu.VMEM((ACT_DEV, width), F32),
            pltpu.VMEM((N_SCEN, QROWS, LANES), F32),
            pltpu.VMEM((COLS, 8, ACT_DEV), F32),
            pltpu.VMEM((5, 32, LANES), F32),
            pltpu.SemaphoreType.DMA((8,)),
            pltpu.SemaphoreType.DMA((COLS - 1,)),
            pltpu.SemaphoreType.DMA((COLS - 1,)),
            pltpu.SemaphoreType.REGULAR,
            pltpu.SemaphoreType.DMA((N_SCEN,)),
            pltpu.SemaphoreType.DMA((N_SCEN,)),
        ],
        compiler_params=pltpu.CompilerParams(
            collective_id=0, has_side_effects=True, vmem_limit_bytes=32 * 2**20
        ),
        name="exchange",
    )(coef, mask.reshape(256, LANES), assign.reshape(32, LANES))

    steps = 8
    per_step = 64 // steps

    def fixed(*shape):
        return pl.BlockSpec(shape, lambda i: (0,) * len(shape))

    return pl.pallas_call(
        functools.partial(place_kernel, per_step),
        out_shape=jax.ShapeDtypeStruct((1, PART, 64 * 512), F32),
        grid=(steps,),
        in_specs=[
            pl.BlockSpec(memory_space=pltpu.SMEM),
            fixed(N_SCEN, QROWS, LANES),
            fixed(8, LANES),
            fixed(4, 64, LANES),
            fixed(4, 64, LANES),
        ],
        out_specs=pl.BlockSpec((1, PART, per_step * 512), lambda i: (0, 0, i)),
        scratch_shapes=[pltpu.VMEM((4 * N_SCEN * HELD, LANES), F32)],
        compiler_params=pltpu.CompilerParams(
            dimension_semantics=("arbitrary",), vmem_limit_bytes=32 * 2**20
        ),
        name="place",
    )(tbl, held, inv, idx, val)


def solution(mesh):
    in_specs = (P("scen", "col"), P(), P())
    out_specs = P("col", "scen", None)
    return jax.shard_map(
        on_device, mesh=mesh, in_specs=in_specs, out_specs=out_specs, check_vma=False
    )
```

time: 223 us -> 95 us (0.43)
  the two profiles are of different devices: /device:TPU:38 before, /device:TPU:1 now
where the time goes in v1:
time: 95 us; the launch traced here: 94.8 us
  Pallas kernels  91 us (96%)
  local copies, waits for them, and re-layouts  3.81 us (4%)
    pallas_call x1, Pallas kernels, on_device(): pl.pallas_call(exchange_kernel, out_shape=(jax.ShapeDtypeStruct((N_SCEN,...  67.6 us
    pallas_call x1, Pallas kernels, on_device(): pl.pallas_call(functools.partial(place_kernel, per_step), out_shape=jax.S...  23.4 us
    unnamed x6, local copies, waits for them, and re-layouts  3.81 us

profile of v1, /device:TPU:1, one launch (start us, length us, event | category | flops | bytes accessed | tf_op | source)
XLA Modules:
  0.0 94.8 jit_solution(13928407106184299883)
XLA Ops:
  0.0 0.0 copy-start
  0.0 2.2 %copy-done = f32[512,2048]{1,0:T(8,128)S(1)} copy-done((f32[512,2048]{1,0:T(8,128)S(1)}, f32[512,2048]{1,0:T(8,128)}, u32[]{:S(2)}) %copy-start) | copy-done | bytes 4194328
  2.2 0.0 copy-start.1
  2.2 0.9 copy-done.1
  3.1 0.0 copy-start.2
  3.1 0.7 copy-done.2
  3.8 67.6 %exchange.1 = (f32[64,64,128]{2,1,0:T(8,128)S(1)}, f32[8,128]{1,0:T(8,128)S(1)}, s32[64,64]{1,0:T(8,128)S(1)}, s32[4,64,128]{2,1,0:T(8,128)S(1)}, f32[4,64,128]{2,1,0:T(8,128)S(1)}) custom-call(f32[512,2048]{1,0:T(8,128)S(1)} %copy-done, s32[256,128]{1,0:T(8,128)S(1)} %bitcast.2, s32[32,128]{1,0:T(8,128)S(1)} %bitcast.3), custom_call_target="tpu_custom_call" | custom-call | tf_op jit(solution)/shard_map/exchange/pallas_call | solution.py:329
  71.4 23.4 %place.1 = f32[1,32,32768]{2,1,0:T(8,128)} custom-call(s32[64,64]{1,0:T(8,128)S(1)} %get-tuple-element.10.tbl_ref, f32[64,64,128]{2,1,0:T(8,128)S(1)} %get-tuple-element.11.held_ref, f32[8,128]{1,0:T(8,128)S(1)} %get-tuple-element.12.inv_ref, s32[4,64,128]{2,1,0:T(8,128)S(1)} %get-tuple-element.13.idx_ref, f32[4,64,128]{2,1,0:T(8,128)S(1)} %get-tuple-element.14.val_ref), custom_call_target="tpu_custom_call" | custom-call | tf_op jit(solution)/shard_map/place/pallas_call | solution.py:366
Async XLA Ops:
  0.0 2.2 %copy-start = (f32[512,2048]{1,0:T(8,128)S(1)}, f32[512,2048]{1,0:T(8,128)}, u32[]{:S(2)}) copy-start(f32[512,2048]{1,0:T(8,128)} %coef_ref.1) | copy-start | bytes 12582916
  2.2 0.9 copy-start.1
  3.1 0.7 copy-start.2

commit v2 on v1

--- a/solution.py
+++ b/solution.py
@@ -43,19 +43,23 @@
 
 def exchange_kernel(
     coef_ref,
-    mask_ref,
-    assign_ref,
-    held_ref,
+    mask_hbm,
+    assign_hbm,
+    turned,
     inv_ref,
     tbl_ref,
     idx_ref,
     val_ref,
     coef_v,
+    mask_ref,
+    assign_ref,
     pick,
     dense,
     packed,
+    recv,
     part,
     slots,
+    small_sem,
     in_sem,
     csend,
     crecv,
@@ -77,8 +81,12 @@
             coef_ref.at[:, cols], coef_v.at[:, cols], in_sem.at[e]
         )
 
+    load_mask = pltpu.make_async_copy(mask_hbm, mask_ref, small_sem.at[0])
+    load_assign = pltpu.make_async_copy(assign_hbm, assign_ref, small_sem.at[1])
+    load_mask.start()
     for e in range(n_chunks):
         load(e).start()
+    load_assign.start()
 
     barrier = pltpu.get_barrier_semaphore()
     across = (me + half) % N_SCEN
@@ -103,6 +111,8 @@
         return 0
 
     lax.fori_loop(1, half, greet, 0)
+
+    load_mask.wait()
 
     own = mask_ref[pl.ds(pl.multiple_of(me // 2 * 8, 8), 8), :].astype(F32)
     own = jnp.where(me % 2 == 1, pltpu.roll(own, 4, 0), own)
@@ -165,7 +175,7 @@
     def send(d):
         return pltpu.make_async_remote_copy(
             src_ref=packed.at[d],
-            dst_ref=held_ref.at[me],
+            dst_ref=recv.at[me],
             send_sem=ssem.at[d],
             recv_sem=rsem.at[me],
             device_id={"scen": d},
@@ -201,7 +211,7 @@
         return 0
 
     lax.fori_loop(0, n_tiles, pack, 0)
-    held_ref[me] = packed[me]
+    recv[me] = packed[me]
 
     count = jnp.zeros((32, LANES), F32)
     bits = jnp.zeros((32, LANES), F32)
@@ -215,6 +225,7 @@
     first = dot(
         count.astype(BF16), ones_where((r_i < l_i) & (r_i // 64 == l_i // 64))
     ).astype(jnp.int32)
+    load_assign.wait()
     to = assign_ref[...]
     source = 2 * iota((32, LANES), 0) + iota((32, LANES), 1) // 64
     quarter = lax.rem(lax.rem(to, 64) // 16 - first // QROWS + 8, 4)
@@ -257,14 +268,18 @@
         def _():
             pltpu.make_async_remote_copy(
                 src_ref=packed.at[s],
-                dst_ref=held_ref.at[s],
+                dst_ref=recv.at[s],
                 send_sem=ssem.at[s],
                 recv_sem=rsem.at[s],
                 device_id={"scen": s},
                 device_id_type=MESH,
             ).wait_recv()
 
-        x = held_ref[s]
+        x = recv[s]
+        tall = jnp.concatenate([x, pltpu.roll(x[:8], LANES - PART, 1)], axis=0)
+        for p in range(4):
+            y = pltpu.roll(tall, PART * p, 1) if p else tall
+            turned[pl.ds(pl.multiple_of((p * N_SCEN + s) * HELD, 8), HELD), :] = y
         return acc + x * x
 
     acc = lax.fori_loop(0, N_SCEN, take, jnp.zeros((QROWS, LANES), F32))
@@ -283,26 +298,12 @@
     lax.fori_loop(1, N_SCEN, finish, 0)
 
 
-def place_kernel(per_step, tbl_ref, held_ref, inv_ref, idx_ref, val_ref, out_ref, turned):
+def place_kernel(per_step, tbl_ref, turned, inv_ref, idx_ref, val_ref, out_ref):
     step = pl.program_id(0)
-
-    @pl.when(step == 0)
-    def _():
-        inv = jnp.broadcast_to(inv_ref[0:1, :], (HELD, LANES))
-
-        def turn(s, _):
-            x = held_ref[s]
-            x = jnp.concatenate([x, pltpu.roll(x[:8], LANES - PART, 1)], axis=0) * inv
-            for p in range(4):
-                y = pltpu.roll(x, PART * p, 1) if p else x
-                turned[pl.ds(pl.multiple_of((p * N_SCEN + s) * HELD, 8), HELD), :] = y
-            return 0
-
-        lax.fori_loop(0, N_SCEN, turn, 0)
-
+    inv = inv_ref[...]
     lane_group = iota((8, LANES), 1) // PART
 
-    def block(h, _):
+    for h in range(per_step):
         hi = step * per_step + h
         tiles = []
         for i in range(16):
@@ -310,40 +311,47 @@
             for q in range(4):
                 x = turned[pl.ds(tbl_ref[hi, 16 * q + i], 8), :]
                 m = x if m is None else jnp.where(lane_group == q, x, m)
-            tiles.append(m)
+            tiles.append(m * inv)
         flipped = jnp.concatenate(tiles, axis=0).T
         for q in range(4):
             idx = jnp.broadcast_to(idx_ref[q, pl.ds(hi, 1), :], (PART, LANES))
             val = jnp.broadcast_to(val_ref[q, pl.ds(hi, 1), :], (PART, LANES))
             y = flipped[q * PART : (q + 1) * PART, :]
             y = jnp.take_along_axis(y, idx, axis=1) * val
-            out_ref[0, :, pl.ds(pl.multiple_of(h * 512 + q * LANES, LANES), LANES)] = y
-        return 0
-
-    lax.fori_loop(0, per_step, block, 0)
+            at = h * 512 + q * LANES
+            out_ref[0, :, at : at + LANES] = y
 
 
 def on_device(coef, mask, assign):
     rows, width = coef.shape
     vmem = pl.BlockSpec(memory_space=pltpu.VMEM)
-    held, inv, tbl, idx, val = pl.pallas_call(
+    hbm = pl.BlockSpec(memory_space=pltpu.HBM)
+
+    def in_hbm(x):
+        return pltpu.with_memory_space_constraint(x, pltpu.HBM)
+
+    turned, inv, tbl, idx, val = pl.pallas_call(
         exchange_kernel,
         out_shape=(
-            jax.ShapeDtypeStruct((N_SCEN, QROWS, LANES), F32),
+            pltpu.VMEM((4 * N_SCEN * HELD, LANES), F32),
             jax.ShapeDtypeStruct((8, LANES), F32),
             jax.ShapeDtypeStruct((64, 64), jnp.int32),
             jax.ShapeDtypeStruct((4, 64, LANES), jnp.int32),
             jax.ShapeDtypeStruct((4, 64, LANES), F32),
         ),
-        in_specs=[pl.BlockSpec(memory_space=pltpu.HBM), vmem, vmem],
+        in_specs=[hbm, hbm, hbm],
         out_specs=(vmem, vmem, vmem, vmem, vmem),
         scratch_shapes=[
             pltpu.VMEM((rows, width), F32),
+            pltpu.VMEM((256, LANES), jnp.int32),
+            pltpu.VMEM((32, LANES), jnp.int32),
             pltpu.VMEM((ACT_DEV, rows), BF16),
             pltpu.VMEM((ACT_DEV, width), F32),
             pltpu.VMEM((N_SCEN, QROWS, LANES), F32),
+            pltpu.VMEM((N_SCEN, QROWS, LANES), F32),
             pltpu.VMEM((COLS, 8, ACT_DEV), F32),
             pltpu.VMEM((5, 32, LANES), F32),
+            pltpu.SemaphoreType.DMA((2,)),
             pltpu.SemaphoreType.DMA((8,)),
             pltpu.SemaphoreType.DMA((COLS - 1,)),
             pltpu.SemaphoreType.DMA((COLS - 1,)),
@@ -352,10 +360,14 @@
             pltpu.SemaphoreType.DMA((N_SCEN,)),
         ],
         compiler_params=pltpu.CompilerParams(
-            collective_id=0, has_side_effects=True, vmem_limit_bytes=32 * 2**20
+            collective_id=0, has_side_effects=True, vmem_limit_bytes=20 * 2**20
         ),
         name="exchange",
-    )(coef, mask.reshape(256, LANES), assign.reshape(32, LANES))
+    )(
+        in_hbm(coef),
+        in_hbm(mask.reshape(256, LANES)),
+        in_hbm(assign.reshape(32, LANES)),
+    )
 
     steps = 8
     per_step = 64 // steps
@@ -369,18 +381,17 @@
         grid=(steps,),
         in_specs=[
             pl.BlockSpec(memory_space=pltpu.SMEM),
-            fixed(N_SCEN, QROWS, LANES),
+            vmem,
             fixed(8, LANES),
             fixed(4, 64, LANES),
             fixed(4, 64, LANES),
         ],
         out_specs=pl.BlockSpec((1, PART, per_step * 512), lambda i: (0, 0, i)),
-        scratch_shapes=[pltpu.VMEM((4 * N_SCEN * HELD, LANES), F32)],
         compiler_params=pltpu.CompilerParams(
-            dimension_semantics=("arbitrary",), vmem_limit_bytes=32 * 2**20
+            dimension_semantics=("arbitrary",), vmem_limit_bytes=16 * 2**20
         ),
         name="place",
-    )(tbl, held, inv, idx, val)
+    )(tbl, turned, inv, idx, val)
 
 
 def solution(mesh):

time: 95 us -> 80.8 us (0.85)
  the two profiles are of different devices: /device:TPU:1 before, /device:TPU:31 now
where the time goes in v2:
time: 80.8 us; the launch traced here: 80.7 us
  Pallas kernels  80.7 us (100%)
    pallas_call x1, Pallas kernels, on_device(): pl.pallas_call(exchange_kernel, out_shape=(pltpu.VMEM((4 * N_SCEN * HELD,...  73.3 us
    pallas_call x1, Pallas kernels, on_device(): pl.pallas_call(functools.partial(place_kernel, per_step), out_shape=jax.S...  7.33 us

profile of v2, /device:TPU:31, one launch (start us, length us, event | category | flops | bytes accessed | tf_op | source)
XLA Modules:
  0.0 80.7 jit_solution(9692236848968240913)
XLA Ops:
  0.0 73.3 %exchange.1 = (f32[18432,128]{1,0:T(8,128)S(1)}, f32[8,128]{1,0:T(8,128)S(1)}, s32[64,64]{1,0:T(8,128)S(1)}, s32[4,64,128]{2,1,0:T(8,128)S(1)}, f32[4,64,128]{2,1,0:T(8,128)S(1)}) custom-call(f32[512,2048]{1,0:T(8,128)} %coef_ref.1, s32[256,128]{1,0:T(8,128)} %bitcast.2, s32[32,128]{1,0:T(8,128)} %bitcast.3), custom_call_target="tpu_custom_call" | custom-call | tf_op jit(solution)/shard_map/exchange/pallas_call | solution.py:333
  73.4 7.3 %place.1 = f32[1,32,32768]{2,1,0:T(8,128)} custom-call(s32[64,64]{1,0:T(8,128)S(1)} %get-tuple-element.10.tbl_ref, f32[18432,128]{1,0:T(8,128)S(1)} %get-tuple-element.11.turned, f32[8,128]{1,0:T(8,128)S(1)} %get-tuple-element.12.inv_ref, s32[4,64,128]{2,1,0:T(8,128)S(1)} %get-tuple-element.13.idx_ref, f32[4,64,128]{2,1,0:T(8,128)S(1)} %get-tuple-element.14.val_ref), custom_call_target="tpu_custom_call" | custom-call | tf_op jit(solution)/shard_map/place/pallas_call | solution.py:378

commit v3 on v2

--- a/solution.py
+++ b/solution.py
@@ -17,6 +17,7 @@
 QROWS = 64
 HELD = QROWS + 8
 N_SCEN = 64
+LAG = 4
 COLS = 4
 MESH = pl.DeviceIdType.MESH
 F32 = jnp.float32
@@ -56,6 +57,7 @@
     pick,
     dense,
     packed,
+    relay,
     recv,
     part,
     slots,
@@ -63,9 +65,12 @@
     in_sem,
     csend,
     crecv,
-    zsem,
+    axis_sem,
+    twin_sem,
     ssem,
     rsem,
+    relay_sem,
+    forward_sem,
 ):
     rows, width = coef_ref.shape
     me = lax.axis_index("scen")
@@ -88,39 +93,34 @@
         load(e).start()
     load_assign.start()
 
+    own = me % half
+    across = (me + half) % N_SCEN
+    own_x, own_y, own_c = own // 8, own // 2 % 4, own % 2
+
+    def index(x, y, c):
+        return x % 4 * 8 + y % 4 * 2 + c % 2
+
+    def signal(sem, device):
+        pl.semaphore_signal(sem, inc=1, device_id=device, device_id_type=MESH)
+
+    along_x = [{"scen": zh * half + index(own_x + d, own_y, own_c)} for d in (1, 2, 3)]
+    along_y = [{"scen": zh * half + index(own_x, own_y + d, own_c)} for d in (1, 2, 3)]
+    twin = {"scen": zh * half + index(own_x, own_y, own_c + 1)}
+    others = [{"col": (group + d) % COLS} for d in range(1, COLS)]
+
     barrier = pltpu.get_barrier_semaphore()
-    across = (me + half) % N_SCEN
-    pl.semaphore_signal(
-        barrier, inc=1, device_id={"scen": across}, device_id_type=MESH
-    )
-    for d in range(1, COLS):
-        pl.semaphore_signal(
-            barrier,
-            inc=1,
-            device_id={"col": (group + d) % COLS},
-            device_id_type=MESH,
-        )
-
-    def greet(t, _):
-        pl.semaphore_signal(
-            barrier,
-            inc=1,
-            device_id={"scen": zh * half + (me + t) % half},
-            device_id_type=MESH,
-        )
-        return 0
-
-    lax.fori_loop(1, half, greet, 0)
+    for device in [{"scen": across}] + others + along_x + along_y + [twin]:
+        signal(barrier, device)
 
     load_mask.wait()
 
-    own = mask_ref[pl.ds(pl.multiple_of(me // 2 * 8, 8), 8), :].astype(F32)
-    own = jnp.where(me % 2 == 1, pltpu.roll(own, 4, 0), own)
+    mine = mask_ref[pl.ds(pl.multiple_of(me // 2 * 8, 8), 8), :].astype(F32)
+    mine = jnp.where(me % 2 == 1, pltpu.roll(mine, 4, 0), mine)
     before = ones_where(iota((LANES, LANES), 0) < iota((LANES, LANES), 1))
-    rank = dot(own.astype(BF16), before)
+    rank = dot(mine.astype(BF16), before)
     base = jnp.zeros((1, 1), F32)
     for k in range(rows // LANES):
-        row = own[k : k + 1, :]
+        row = mine[k : k + 1, :]
         here = (rank[k : k + 1, :] + base).astype(jnp.int32)
         here = jnp.where(row > 0.5, here, -1)
         pick[:, k * LANES : (k + 1) * LANES] = ones_where(
@@ -145,10 +145,10 @@
         return acc
 
     acc = lax.fori_loop(0, n_chunks, compact, jnp.zeros((ACT_DEV, LANES), F32))
-    mine = jnp.sum(acc.T, axis=0, keepdims=True)
-    part[group] = jnp.broadcast_to(mine, (8, ACT_DEV))
-
-    pl.semaphore_wait(barrier, half - 1 + 1 + COLS - 1)
+    sums = jnp.sum(acc.T, axis=0, keepdims=True)
+    part[group] = jnp.broadcast_to(sums, (8, ACT_DEV))
+
+    pl.semaphore_wait(barrier, 11)
 
     def share(d):
         return pltpu.make_async_remote_copy(
@@ -162,32 +162,17 @@
 
     for d in range(1, COLS):
         share(d).start()
-    pl.semaphore_signal(zsem, inc=1, device_id={"scen": across}, device_id_type=MESH)
+    for device in along_x + [twin]:
+        signal(axis_sem, device)
     for d in range(1, COLS):
         share(d).wait()
     total = part[0] + part[1] + part[2] + part[3]
     inv_row = 1.0 / jnp.sqrt(total[0:1, :] / NV + EPS)
     scale = jnp.broadcast_to(inv_row, (LANES, ACT_DEV)).T
-    pl.semaphore_wait(zsem, 1)
 
     lane_group = iota((QROWS, LANES), 1) // PART
 
-    def send(d):
-        return pltpu.make_async_remote_copy(
-            src_ref=packed.at[d],
-            dst_ref=recv.at[me],
-            send_sem=ssem.at[d],
-            recv_sem=rsem.at[me],
-            device_id={"scen": d},
-            device_id_type=MESH,
-        )
-
-    n_tiles = width // LANES
-    half_tiles = n_tiles // 2
-    own_tile = (me % half) // 4
-
-    def pack(i, _):
-        e = ((1 - zh + i // half_tiles) % 2) * half_tiles + (own_tile + i) % half_tiles
+    def pack(e):
         cols = pl.ds(pl.multiple_of(e * LANES, LANES), LANES)
         quarters = [
             dense[q * QROWS : (q + 1) * QROWS, cols]
@@ -201,16 +186,103 @@
                 moved = pltpu.roll(quarters[q], shift, 1) if shift else quarters[q]
                 out = moved if out is None else jnp.where(lane_group == q, moved, out)
             packed[4 * e + f] = out
-        for f in range(4):
-            d = 4 * e + (f + me) % 4
-
-            @pl.when(d != me)
-            def _():
-                send(d).start()
+
+    def offset(i):
+        late = i // 2
+        return (1 - late) * (2 - i) + late * (9 - 3 * i)
+
+    def ahead(k):
+        return index(
+            own_x + offset(k // 8), own_y + offset(k // 2 % 4), own_c + 1 - k % 2
+        )
+
+    def behind(k):
+        return index(
+            own_x + 4 - offset(k // 8), own_y + 4 - offset(k // 2 % 4), own_c + 1 - k % 2
+        )
+
+    def to_relay(j):
+        return pltpu.make_async_remote_copy(
+            src_ref=packed.at[(1 - zh) * half + j],
+            dst_ref=relay.at[j],
+            send_sem=ssem.at[(1 - zh) * half + j],
+            recv_sem=relay_sem.at[j],
+            device_id={"scen": across},
+            device_id_type=MESH,
+        )
+
+    def direct(d):
+        return pltpu.make_async_remote_copy(
+            src_ref=packed.at[d],
+            dst_ref=recv.at[me],
+            send_sem=ssem.at[d],
+            recv_sem=rsem.at[me],
+            device_id={"scen": d},
+            device_id_type=MESH,
+        )
+
+    def forward(j):
+        return pltpu.make_async_remote_copy(
+            src_ref=relay.at[j],
+            dst_ref=recv.at[across],
+            send_sem=forward_sem.at[j],
+            recv_sem=rsem.at[across],
+            device_id={"scen": zh * half + j},
+            device_id_type=MESH,
+        )
+
+    def arrival(s):
+        return pltpu.make_async_remote_copy(
+            src_ref=packed.at[s],
+            dst_ref=recv.at[s],
+            send_sem=ssem.at[s],
+            recv_sem=rsem.at[s],
+            device_id={"scen": s},
+            device_id_type=MESH,
+        )
+
+    last = half - 1
+
+    def send_far(i, _):
+        x = (own_x + offset(i)) % 4
+        for p in range(2):
+            pack((1 - zh) * 8 + x * 2 + p)
+        for j in range(8):
+            k = 8 * i + j
+            if j < 7:
+                to_relay(ahead(k)).start()
+            else:
+
+                @pl.when(k < last)
+                def _():
+                    to_relay(ahead(k)).start()
 
         return 0
 
-    lax.fori_loop(0, n_tiles, pack, 0)
+    lax.fori_loop(0, 4, send_far, 0)
+    direct(across).start()
+
+    pl.semaphore_wait(axis_sem, 4)
+    signal(twin_sem, twin)
+    pl.semaphore_wait(twin_sem, 1)
+
+    def send_near(i, _):
+        x = (own_x + offset(i)) % 4
+        for p in range(2):
+            pack(zh * 8 + x * 2 + p)
+        for j in range(8):
+            k = 8 * i + j
+            if j < 7:
+                direct(zh * half + ahead(k)).start()
+            else:
+
+                @pl.when(k < last)
+                def _():
+                    direct(zh * half + ahead(k)).start()
+
+        return 0
+
+    lax.fori_loop(0, 4, send_near, 0)
     recv[me] = packed[me]
 
     count = jnp.zeros((32, LANES), F32)
@@ -261,20 +333,7 @@
         idx_ref[q] = iota((64, LANES), 1) - k_i + before_k
         val_ref[q] = own_bit.astype(F32)
 
-    def take(t, acc):
-        s = (me + t) % N_SCEN
-
-        @pl.when(t > 0)
-        def _():
-            pltpu.make_async_remote_copy(
-                src_ref=packed.at[s],
-                dst_ref=recv.at[s],
-                send_sem=ssem.at[s],
-                recv_sem=rsem.at[s],
-                device_id={"scen": s},
-                device_id_type=MESH,
-            ).wait_recv()
-
+    def take(s, acc):
         x = recv[s]
         tall = jnp.concatenate([x, pltpu.roll(x[:8], LANES - PART, 1)], axis=0)
         for p in range(4):
@@ -282,20 +341,47 @@
             turned[pl.ds(pl.multiple_of((p * N_SCEN + s) * HELD, 8), HELD), :] = y
         return acc + x * x
 
-    acc = lax.fori_loop(0, N_SCEN, take, jnp.zeros((QROWS, LANES), F32))
+    def pass_on(k):
+        j = ahead(k)
+        to_relay(j).wait_recv()
+        forward(j).start()
+
+    def from_near(k, acc):
+        s = zh * half + behind(k)
+        arrival(s).wait_recv()
+        return take(s, acc)
+
+    def from_far(k, acc):
+        s = (1 - zh) * half + behind(k)
+        arrival(s).wait_recv()
+        return take(s, acc)
+
+    def early(k, acc):
+        pass_on(k)
+        return from_near(k, acc)
+
+    def steady(k, acc):
+        pass_on(k)
+        return from_far(k - LAG, from_near(k, acc))
+
+    acc = take(me, jnp.zeros((QROWS, LANES), F32))
+    acc = lax.fori_loop(0, LAG, early, acc)
+    acc = lax.fori_loop(LAG, last, steady, acc)
+    acc = lax.fori_loop(last - LAG, half, from_far, acc)
     col = jnp.sum(acc, axis=0, keepdims=True)
     col = jnp.broadcast_to(col, (8, LANES))
     col = col + pltpu.roll(col, 64, 1)
     col = col + pltpu.roll(col, 32, 1)
     inv_ref[...] = 1.0 / jnp.sqrt(col / (ACT_DEV * N_SCEN) + EPS)
 
-    def finish(t, _):
-        d = (me + t) % N_SCEN
-
-        send(d).wait_send()
+    def finish(j, _):
+        to_relay(ahead(j)).wait_send()
+        forward(ahead(j)).wait_send()
+        direct(zh * half + ahead(j)).wait_send()
         return 0
 
-    lax.fori_loop(1, N_SCEN, finish, 0)
+    lax.fori_loop(0, last, finish, 0)
+    direct(across).wait_send()
 
 
 def place_kernel(per_step, tbl_ref, turned, inv_ref, idx_ref, val_ref, out_ref):
@@ -348,6 +434,7 @@
             pltpu.VMEM((ACT_DEV, rows), BF16),
             pltpu.VMEM((ACT_DEV, width), F32),
             pltpu.VMEM((N_SCEN, QROWS, LANES), F32),
+            pltpu.VMEM((N_SCEN // 2, QROWS, LANES), F32),
             pltpu.VMEM((N_SCEN, QROWS, LANES), F32),
             pltpu.VMEM((COLS, 8, ACT_DEV), F32),
             pltpu.VMEM((5, 32, LANES), F32),
@@ -356,8 +443,11 @@
             pltpu.SemaphoreType.DMA((COLS - 1,)),
             pltpu.SemaphoreType.DMA((COLS - 1,)),
             pltpu.SemaphoreType.REGULAR,
+            pltpu.SemaphoreType.REGULAR,
             pltpu.SemaphoreType.DMA((N_SCEN,)),
             pltpu.SemaphoreType.DMA((N_SCEN,)),
+            pltpu.SemaphoreType.DMA((N_SCEN // 2,)),
+            pltpu.SemaphoreType.DMA((N_SCEN // 2,)),
         ],
         compiler_params=pltpu.CompilerParams(
             collective_id=0, has_side_effects=True, vmem_limit_bytes=20 * 2**20

time: 80.8 us -> 75.7 us (0.937)
  the two profiles are of different devices: /device:TPU:31 before, /device:TPU:38 now
where the time goes in v3:
time: 75.7 us; the launch traced here: 75.2 us
  Pallas kernels  75.2 us (99%)
    pallas_call x1, Pallas kernels, on_device(): pl.pallas_call(exchange_kernel, out_shape=(pltpu.VMEM((4 * N_SCEN * HELD,...  67.8 us
    pallas_call x1, Pallas kernels, on_device(): pl.pallas_call(functools.partial(place_kernel, per_step), out_shape=jax.S...  7.33 us

profile of v3, /device:TPU:38, one launch (start us, length us, event | category | flops | bytes accessed | tf_op | source)
XLA Modules:
  0.0 75.2 jit_solution(2920721663730209558)
XLA Ops:
  0.0 67.8 %exchange.1 = (f32[18432,128]{1,0:T(8,128)S(1)}, f32[8,128]{1,0:T(8,128)S(1)}, s32[64,64]{1,0:T(8,128)S(1)}, s32[4,64,128]{2,1,0:T(8,128)S(1)}, f32[4,64,128]{2,1,0:T(8,128)S(1)}) custom-call(f32[512,2048]{1,0:T(8,128)} %coef_ref.1, s32[256,128]{1,0:T(8,128)} %bitcast.2, s32[32,128]{1,0:T(8,128)} %bitcast.3), custom_call_target="tpu_custom_call" | custom-call | tf_op jit(solution)/shard_map/exchange/pallas_call | solution.py:419
  67.8 7.3 %place.1 = f32[1,32,32768]{2,1,0:T(8,128)} custom-call(s32[64,64]{1,0:T(8,128)S(1)} %get-tuple-element.10.tbl_ref, f32[18432,128]{1,0:T(8,128)S(1)} %get-tuple-element.11.turned, f32[8,128]{1,0:T(8,128)S(1)} %get-tuple-element.12.inv_ref, s32[4,64,128]{2,1,0:T(8,128)S(1)} %get-tuple-element.13.idx_ref, f32[4,64,128]{2,1,0:T(8,128)S(1)} %get-tuple-element.14.val_ref), custom_call_target="tpu_custom_call" | custom-call | tf_op jit(solution)/shard_map/place/pallas_call | solution.py:468

commit v4 on v3

--- a/solution.py
+++ b/solution.py
@@ -133,11 +133,9 @@
         cols = pl.ds(pl.multiple_of(e * chunk, chunk), chunk)
         x = coef_v[:, cols]
         hi = x.astype(BF16)
-        rest = x - hi.astype(F32)
-        mid = rest.astype(BF16)
-        low = (rest - mid.astype(F32)).astype(BF16)
+        low = (x - hi.astype(F32)).astype(BF16)
         sel = pick[...]
-        z = dot(sel, hi) + dot(sel, mid) + dot(sel, low)
+        z = dot(sel, hi) + dot(sel, low)
         dense[:, cols] = z
         for j in range(chunk // LANES):
             zj = z[:, j * LANES : (j + 1) * LANES]
@@ -459,7 +457,7 @@
         in_hbm(assign.reshape(32, LANES)),
     )
 
-    steps = 8
+    steps = 4
     per_step = 64 // steps
 
     def fixed(*shape):

time: 75.7 us -> 74.1 us (0.979)
  Pallas kernels: 75.2 us -> 73.4 us
    pallas_call x1, Pallas kernels: 7.33 us -> 6.44 us  [on_device(): pl.pallas_call(functools.partial(place_kernel, per_step), out_shape=jax.S...]
    pallas_call x1, Pallas kernels: 67.8 us -> 66.9 us  [on_device(): pl.pallas_call(exchange_kernel, out_shape=(pltpu.VMEM((4 * N_SCEN * HELD,...]
where the time goes in v4:
time: 74.1 us; the launch traced here: 73.4 us
  Pallas kernels  73.4 us (99%)
    pallas_call x1, Pallas kernels, on_device(): pl.pallas_call(exchange_kernel, out_shape=(pltpu.VMEM((4 * N_SCEN * HELD,...  66.9 us
    pallas_call x1, Pallas kernels, on_device(): pl.pallas_call(functools.partial(place_kernel, per_step), out_shape=jax.S...  6.44 us

profile of v4, /device:TPU:38, one launch (start us, length us, event | category | flops | bytes accessed | tf_op | source)
XLA Modules:
  0.0 73.4 jit_solution(853490644171877)
XLA Ops:
  0.0 66.9 %exchange.1 = (f32[18432,128]{1,0:T(8,128)S(1)}, f32[8,128]{1,0:T(8,128)S(1)}, s32[64,64]{1,0:T(8,128)S(1)}, s32[4,64,128]{2,1,0:T(8,128)S(1)}, f32[4,64,128]{2,1,0:T(8,128)S(1)}) custom-call(f32[512,2048]{1,0:T(8,128)} %coef_ref.1, s32[256,128]{1,0:T(8,128)} %bitcast.2, s32[32,128]{1,0:T(8,128)} %bitcast.3), custom_call_target="tpu_custom_call" | custom-call | tf_op jit(solution)/shard_map/exchange/pallas_call | solution.py:417
  67.0 6.4 %place.1 = f32[1,32,32768]{2,1,0:T(8,128)} custom-call(s32[64,64]{1,0:T(8,128)S(1)} %get-tuple-element.10.tbl_ref, f32[18432,128]{1,0:T(8,128)S(1)} %get-tuple-element.11.turned, f32[8,128]{1,0:T(8,128)S(1)} %get-tuple-element.12.inv_ref, s32[4,64,128]{2,1,0:T(8,128)S(1)} %get-tuple-element.13.idx_ref, f32[4,64,128]{2,1,0:T(8,128)S(1)} %get-tuple-element.14.val_ref), custom_call_target="tpu_custom_call" | custom-call | tf_op jit(solution)/shard_map/place/pallas_call | solution.py:466
